TPU v7x, 32 devices: a whole 2x2x4 slice. The times are simulated.
32 devices in a mesh: row: 4 (over z), col: 8 (over y, x, core).
Axes of the slice: x: 2, y: 2, z: 4, core: 2. Of those that a mesh axis runs over, the one named last changes fastest.
Arguments:
- front: float32 [12288, 12288], P('row', 'col'), as said below
- structure: int32 [3, 96], replicated, may hold values from 0 to 1, as said below
- factor_front: float32 [3, 12288, 512], P(None, 'row', 'col'), may hold values from -0.0546875 to 0.0546875
- factor_border: float32 [2, 512, 512], replicated, may hold values from -0.6 to 0.6
- pivot_inverse: float32 [3, 512, 512], P(None, 'row')
Outputs:
- inverse_front: float32 [3, 512, 12288], P(None, 'row', 'col')
- inverse_parent: float32 [2, 512, 512], P(None, 'row')
- inverse_diagonal: float32 [3, 512, 512], P(None, 'row')
Inputs may be any that keep to these rules, and one draw needn't show every extreme that they name: front is exactly symmetric. structure[k, b] = 1 where front block b (rows b * 128 to (b + 1) * 128 - 1) lies in supernode k's structure; every 1 in row k is also a 1 in row k - 1; blocks b < 24 are 1 in every row.
All inputs are finite; a program needn't handle non-finite values.
Results may differ from a plain program's by a relative error of at most 0.0001.
Values sent between devices are 32-bit elements; how exact they have to be, the bound alone decides.
No kernel may reach another device: no remote copies, remote signals or barrier semaphores. Data moves between devices by JAX's collectives and lax.ppermute only.
A program may use at most 128 MiB of HBM per device.

v0:
```python
import jax
import jax.numpy as jnp
from jax import lax
from jax.sharding import PartitionSpec as P

BLK = 128


HIGH = lax.Precision.HIGHEST


def broadcast(x, axis, root):
    mine = lax.axis_index(axis) == root
    return lax.psum(jnp.where(mine, x, jnp.zeros_like(x)), axis)


def matmul(former, latter):
    return jnp.dot(former, latter, precision=HIGH, preferred_element_type=jnp.float32)


def contract_first(former, latter):
    return lax.dot_general(
        former, latter, (((0,), (0,)), ((), ())), precision=HIGH, preferred_element_type=jnp.float32
    )


def block_flags(structure_row, first_row, rows_count):
    position = first_row + jnp.arange(rows_count, dtype=jnp.int32)
    owners = position // BLK
    numbers = jnp.arange(structure_row.shape[0], dtype=jnp.int32)
    matches = (owners[:, None] == numbers[None, :]).astype(jnp.float32)
    return jnp.dot(matches, structure_row.astype(jnp.float32), precision=HIGH)


def body(front, structure, factor_front, factor_border, pivot_inverse):
    row_index = lax.axis_index("row")
    col_index = lax.axis_index("col")
    rows_here = front.shape[0]
    cols_here = front.shape[1]
    width_here = pivot_inverse.shape[1]
    supers = structure.shape[0]
    row_first = row_index * rows_here
    col_first = col_index * cols_here
    fronts = []
    parents = []
    diagonals = []
    previous = None
    diag_prev = None
    for section in range(supers):
        gathered = lax.all_gather(factor_front[section], "col", axis=1, tiled=True)
        row_flags = block_flags(structure[section], row_first, rows_here)
        factor_rows = gathered * row_flags[:, None]
        own_half = lax.dynamic_slice_in_dim(factor_rows, col_index % 2 * cols_here, cols_here, 0)
        factor_cols = broadcast(own_half, "row", col_index // 2)
        partial_value = contract_first(factor_rows, front)
        if section > 0:
            border = factor_border[section - 1]
            border_rows = lax.dynamic_slice_in_dim(border, row_index * width_here, width_here, 0)
            partial_value = partial_value + contract_first(border_rows, previous)
            parent_part = lax.psum(matmul(previous, factor_cols), "col")
            parent_rows = parent_part + matmul(diag_prev, border)
            parent_all = lax.all_gather(parent_rows, "row", axis=0, tiled=True)
            parents.append(-parent_rows)
        image_rows = lax.psum_scatter(partial_value, "row", scatter_dimension=0, tiled=True)
        col_flags = block_flags(structure[section], col_first, cols_here)
        current = -(image_rows * col_flags[None, :])
        gram_rows = lax.psum(matmul(image_rows, factor_cols), "col")
        diag_now = pivot_inverse[section] + gram_rows
        if section > 0:
            parent_slice = lax.dynamic_slice_in_dim(
                parent_all, row_index * width_here, width_here, 1
            )
            diag_now = diag_now + contract_first(parent_slice, border)
        fronts.append(current)
        diagonals.append(diag_now)
        previous = current
        diag_prev = diag_now
    return (jnp.stack(fronts), jnp.stack(parents), jnp.stack(diagonals))


def solution(mesh):
    placed = (P("row", "col"), P(), P(None, "row", "col"), P(), P(None, "row", None))
    return jax.shard_map(
        body,
        mesh=mesh,
        in_specs=placed,
        out_specs=(P(None, "row", "col"), P(None, "row", None), P(None, "row", None)),
        check_vma=False,
    )
```

profile of v0, /device:TPU:0, one launch (start us, length us, event | category | flops | bytes accessed | tf_op | source)
XLA Modules:
  0.0 802.7 jit_solution(8092300581253794925)
XLA Ops:
  7.2 3.1 fusion.61
  13.2 45.4 %all-gather.13.cloned.1.call-done = f32[1,3072,512]{1,2,0:T(8,128)} async-done(((f32[1,3072,64]{1,2,0:T(8,128)}), f32[1,3072,512]{1,2,0:T(8,128)}) %all-gather.13.cloned.1.call-update) | async-done | bytes 6291472 | tf_op jit(solution)/shard_map/all_gather | solution.py:50
  58.6 3.4 bitcast_multiply_fusion.2
  62.0 2.6 copy-done.1
  64.7 33.4 %fusion.63 = f32[512,1536]{1,0:T(8,128)} fusion(f32[3072,512]{0,1:T(8,128)S(1)} %bitcast_multiply_fusion.2, f32[3072,1536]{1,0:T(8,128)} %param.5), kind=kOutput, calls=%fused_computation.103 | convolution fusion | flops 28991029248 | bytes 28311552 | tf_op jit(solution)/shard_map/dot_general | solution.py:22
  102.7 3.2 all-gather.15.cloned.1.call-done
  105.9 3.4 bitcast_multiply_fusion.1
  109.3 2.6 copy-done.2
  111.9 33.4 %fusion.64 = f32[512,1536]{1,0:T(8,128)} fusion(f32[3072,512]{0,1:T(8,128)S(1)} %bitcast_multiply_fusion.1, f32[3072,1536]{1,0:T(8,128)} %param.5), kind=kOutput, calls=%fused_computation.104 | convolution fusion | flops 28991029248 | bytes 28311552 | tf_op jit(solution)/shard_map/dot_general | solution.py:22
  145.3 23.4 %reduce-scatter.4.cloned.1.call-done = f32[128,1536]{1,0:T(8,128)} async-done(((f32[512,1536]{1,0:T(8,128)}), f32[128,1536]{1,0:T(8,128)}) %reduce-scatter.4.cloned.1.call-update) | async-done | bytes 786448 | tf_op jit(solution)/shard_map/reduce_scatter | solution.py:64
  168.6 6.6 convolution_add_fusion.1
  177.6 4.1 dynamic-slice_select_fusion.2
  181.6 3.8 dynamic-slice_select_fusion.1
  185.4 30.3 %all-gather.17.cloned.1.call-done = f32[1,3072,512]{1,2,0:T(8,128)} async-done(((f32[1,3072,64]{1,2,0:T(8,128)}), f32[1,3072,512]{1,2,0:T(8,128)}) %all-gather.17.cloned.1.call-update) | async-done | bytes 6291472 | tf_op jit(solution)/shard_map/all_gather | solution.py:50
  215.7 3.4 bitcast_multiply_fusion
  219.1 2.6 copy-done.3
  224.4 35.4 %fusion.65 = f32[512,1536]{1,0:T(8,128)} fusion(f32[3072,512]{0,1:T(8,128)} %copy-done.3, f32[3072,1536]{1,0:T(8,128)} %param.5), kind=kOutput, calls=%fused_computation.105 | convolution fusion | flops 28991029248 | bytes 28311552 | tf_op jit(solution)/shard_map/dot_general | solution.py:22
  259.8 18.5 %reduce-scatter.6.cloned.1.call-done = f32[128,1536]{1,0:T(8,128)} async-done(((f32[512,1536]{1,0:T(8,128)}), f32[128,1536]{1,0:T(8,128)}) %reduce-scatter.6.cloned.1.call-update) | async-done | bytes 786448 | tf_op jit(solution)/shard_map/reduce_scatter | solution.py:64
  278.3 5.6 convolution_add_fusion
  284.4 321.2 %all-reduce.7.cloned.1.call-done = (f32[1536,512]{0,1:T(8,128)}, f32[1536,512]{0,1:T(8,128)}, f32[1536,512]{0,1:T(8,128)}) async-done(((f32[1536,512]{0,1:T(8,128)}, f32[1536,512]{0,1:T(8,128)}, f32[1536,512]{0,1:T(8,128)}), (f32[1536,512]{0,1:T(8,128)}, f32[1536,512]{0,1:T(8,128)}, f32[1536,512]{0,1:T(8,128)})) %all-reduce.7.cloned.1.call-update) | async-done | bytes 9437200 | tf_op jit(solution)/shard_map/psum | solution.py:14
  605.6 6.0 fusion.66
  611.6 3.9 fusion.11
  615.5 4.0 fusion.67
  619.5 3.9 fusion.13
  623.4 43.9 %reduce-scatter.8.cloned.1.call-done = f32[128,1536]{1,0:T(8,128)} async-done(((f32[512,1536]{1,0:T(8,128)}), f32[128,1536]{1,0:T(8,128)}) %reduce-scatter.8.cloned.1.call-update) | async-done | bytes 786448 | tf_op jit(solution)/shard_map/reduce_scatter | solution.py:64
  667.3 6.1 fusion.68
  673.7 58.6 %all-reduce.5.cloned.1.call-done = (f32[128,512]{1,0:T(8,128)}, f32[128,512]{1,0:T(8,128)}, f32[128,512]{1,0:T(8,128)}, f32[128,512]{1,0:T(8,128)}, f32[128,512]{1,0:T(8,128)}) async-done(((f32[128,512]{1,0:T(8,128)}, f32[128,512]{1,0:T(8,128)}, f32[128,512]{1,0:T(8,128)}, f32[128,512]{1,0:T(8,128)}, f32[128,512]{1,0:T(8,128)}), (f32[128,512]{1,0:T(8,128)}, f32[128,512]{1,0:T(8,128)}, f32[128,512]{1,0:T(8,128)}, ...) | async-done | bytes 1310736 | tf_op jit(solution)/shard_map/psum | solution.py:60
  732.3 2.5 convolution_add_fusion.5
  736.5 2.2 fusion.14
  738.7 23.4 %all-gather.9.cloned.1.call-done = f32[512,512]{1,0:T(8,128)} async-done(((f32[128,512]{1,0:T(8,128)}), f32[512,512]{1,0:T(8,128)}) %all-gather.9.cloned.1.call-update) | async-done | bytes 1048592 | tf_op jit(solution)/shard_map/all_gather | solution.py:62
  765.5 3.0 pad_maximum_fusion
  770.5 22.5 %all-gather.11.cloned.1.call-done = f32[512,512]{1,0:T(8,128)} async-done(((f32[128,512]{1,0:T(8,128)}), f32[512,512]{1,0:T(8,128)}) %all-gather.11.cloned.1.call-update) | async-done | bytes 1048592 | tf_op jit(solution)/shard_map/all_gather | solution.py:62
  (67 shorter events, 22.6 us)
Async XLA Ops:
  7.2 4.0 copy-start.14
  7.2 51.4 %all-gather.13.cloned.1.call-start = ((), (), s32[]{:S(2)}) async-start(), calls=%async_computation.8 | async-start | bytes 7077888 | tf_op jit(solution)/shard_map/all_gather | solution.py:50
  10.3 95.6 %all-gather.15.cloned.1.call-start = ((), (), s32[]{:S(2)}) async-start(), calls=%async_computation.9 | async-start | bytes 7077888 | tf_op jit(solution)/shard_map/all_gather | solution.py:50
  11.1 157.6 %reduce-scatter.4.cloned.1.call-start = ((), (), s32[]{:S(2)}) async-start(), calls=%async_computation.3 | async-start | bytes 3932160 | tf_op jit(solution)/shard_map/reduce_scatter | solution.py:64
  62.0 2.7 copy-start.1
  98.0 3.5 copy-start
  98.1 117.6 %all-gather.17.cloned.1.call-start = ((), (), s32[]{:S(2)}) async-start(), calls=%async_computation.10 | async-start | bytes 7077888 | tf_op jit(solution)/shard_map/all_gather | solution.py:50
  98.6 179.6 %reduce-scatter.6.cloned.1.call-start = ((), (), s32[]{:S(2)}) async-start(), calls=%async_computation.4 | async-start | bytes 3932160 | tf_op jit(solution)/shard_map/reduce_scatter | solution.py:64
  109.3 2.6 copy-start.2
  175.3 430.3 %all-reduce.7.cloned.1.call-start = ((), (), s32[]{:S(2)}) async-start(), calls=%async_computation.12 | async-start | bytes 18874368 | tf_op jit(solution)/shard_map/psum | solution.py:14
  219.1 2.7 copy-start.3
  223.7 443.5 %reduce-scatter.8.cloned.1.call-start = ((), (), s32[]{:S(2)}) async-start(), calls=%async_computation.5 | async-start | bytes 3932160 | tf_op jit(solution)/shard_map/reduce_scatter | solution.py:64
  283.9 321.7 %copy-start.4 = (f32[128,1536]{1,0:T(8,128)S(1)}, f32[128,1536]{1,0:T(8,128)}, u32[]{:S(2)}) copy-start(f32[128,1536]{1,0:T(8,128)} %reduce-scatter.4.cloned.1.call-done) | copy-start | bytes 2359300
  284.0 448.4 %all-reduce.5.cloned.1.call-start = ((), (), s32[]{:S(2)}) async-start(), calls=%async_computation.11 | async-start | bytes 2621440 | tf_op jit(solution)/shard_map/psum | solution.py:60
  605.6 6.0 copy-start.7
  611.6 3.9 copy-start.5
  615.5 4.0 copy-start.6
  673.4 88.6 %all-gather.9.cloned.1.call-start = ((), (), s32[]{:S(2)}) async-start(), calls=%async_computation.6 | async-start | bytes 1310720 | tf_op jit(solution)/shard_map/all_gather | solution.py:62
  734.8 29.1 %copy-start.13 = (f32[128,512]{1,0:T(8,128)S(1)}, f32[128,512]{1,0:T(8,128)}, u32[]{:S(2)}) copy-start(f32[128,512]{1,0:T(8,128)} %get-tuple-element.3) | copy-start | bytes 786436
  734.9 58.1 %all-gather.11.cloned.1.call-start = ((), (), s32[]{:S(2)}) async-start(), calls=%async_computation.7 | async-start | bytes 1310720 | tf_op jit(solution)/shard_map/all_gather | solution.py:62
  736.5 28.9 %copy-start.8 = (f32[128,1536]{1,0:T(8,128)S(1)}, f32[128,1536]{1,0:T(8,128)}, u32[]{:S(2)}) copy-start(f32[128,1536]{1,0:T(8,128)} %reduce-scatter.8.cloned.1.call-done) | copy-start | bytes 2359300
  765.4 3.1 copy-start.10
  765.4 3.1 copy-start.11
  765.5 4.0 copy-start.9
  765.5 27.4 %copy-start.12 = (f32[128,512]{1,0:T(8,128)S(1)}, f32[128,512]{1,0:T(8,128)}, u32[]{:S(2)}) copy-start(f32[128,512]{1,0:T(8,128)} %get-tuple-element.7) | copy-start | bytes 786436
Sparse Core Ops, SparseCore 0:
  10.5 48.1 all-gather.12
  60.5 45.3 all-gather.14
  108.2 60.3 reduce-scatter.3
  170.4 45.2 all-gather.16
  217.9 60.3 reduce-scatter.5
  281.0 324.5 all-reduce.6
  607.9 59.3 reduce-scatter.7
  673.6 58.6 all-reduce.4
  735.0 27.0 all-gather.8
  765.5 27.3 all-gather.10
where the time goes:
time: 809 us; the launch traced here: 803 us
  waiting for transfers between devices  592 us (73%)
  matrix products  154 us (19%)
  other arithmetic  29.1 us (4%)
  between operations  14.6 us (2%)
  local copies, waits for them, and re-layouts  12.1 us (1%)
    psum x1, waiting for transfers between devices, broadcast(): return lax.psum(jnp.where(mine, x, jnp.zeros_like(x)), axis)  321 us
    dot_general x7, matrix products, contract_first(): lax.dot_general(former, latter, (((0,), (0,)), ((), ())), precision=HIGH,...  118 us
    reduce_scatter x3, waiting for transfers between devices, body(): lax.psum_scatter(partial_value, 'row', scatter_dimension=0, tiled=True)  85.7 us
    all_gather x3, waiting for transfers between devices, body(): gathered = lax.all_gather(factor_front[section], 'col', axis=1, tiled=True)  79 us
    psum x1, waiting for transfers between devices, body(): parent_part = lax.psum(matmul(previous, factor_cols), 'col')  58.6 us
    all_gather x2, waiting for transfers between devices, body(): parent_all = lax.all_gather(parent_rows, 'row', axis=0, tiled=True)  45.9 us
    dot_general x7, matrix products, matmul(): jnp.dot(former, latter, precision=HIGH, preferred_element_type=jnp.float32)  27.9 us
  transfers between devices with their start and end apart: 10, of which 10 were waited for; matrix products, arithmetic and copies ran while one was open for 21% of the time, Pallas kernels for 0%

commit v1 on v0

v1 whole, which is shorter than its diff:
```python
import jax
import jax.numpy as jnp
from jax import lax
from jax.sharding import PartitionSpec as P


BLK = 128
HALVES = 2

HIGH = lax.Precision.HIGH


def contract(former, latter, former_dim, latter_dim):
    return lax.dot_general(
        former,
        latter,
        (((former_dim,), (latter_dim,)), ((), ())),
        precision=HIGH,
        preferred_element_type=jnp.float32,
    )


def swap(x, axis, bit):
    size = lax.axis_size(axis)
    return lax.ppermute(x, axis, [(i, i ^ bit) for i in range(size)])


def bits_of(size):
    return [1 << i for i in range(size.bit_length() - 1)]


def local_flags(structure, index, count):
    blocks = count // BLK
    mine = lax.dynamic_slice_in_dim(structure, index * blocks, blocks, 1)
    mine = mine.astype(jnp.float32)[:, :, None]
    return jnp.broadcast_to(mine, mine.shape[:2] + (BLK,)).reshape(structure.shape[0], count)


def absolute(pieces, index):
    pieces = [p[None] for p in pieces]
    bit = 1
    while len(pieces) > 1:
        mine = (index // bit) % 2 == 1
        pieces = [
            jnp.concatenate([jnp.where(mine, h, l), jnp.where(mine, l, h)], axis=0)
            for l, h in zip(pieces[::2], pieces[1::2])
        ]
        bit *= 2
    return pieces[0]


def relay(x, axis):
    index = lax.axis_index(axis)
    x = x[None]
    for bit in bits_of(lax.axis_size(axis)):
        got = swap(x, axis, bit)
        mine = (index // bit) % 2 == 1
        x = jnp.concatenate([jnp.where(mine, got, x), jnp.where(mine, x, got)], axis=0)
    return x


def direct(x, axis, join):
    size = lax.axis_size(axis)
    even = [x] + [swap(x, axis, k) for k in range(2, size, 2)]
    even = jnp.concatenate(even, axis=join)
    return even, swap(even, axis, 1)


def quick(x, axis):
    size = lax.axis_size(axis)
    if size != 8:
        even, odd = direct(x[None], axis, 0)
        return [(even, odd)[j % 2][j // 2] for j in range(size)]
    cut = x.shape[0] // 2
    near = {0: x}
    for k in (2, 4):
        near[k] = swap(x, axis, k)
    sides = {1: swap(x, axis, 1)}
    near[6] = jnp.concatenate(
        [swap(near[4][:cut], axis, 2), swap(near[2][cut:], axis, 4)], axis=0
    )
    for k in (2, 4, 6):
        sides[k + 1] = swap(near[k], axis, 1)
    near.update(sides)
    return [near[k] for k in range(size)]


def scatter_sum(x, axis):
    index = lax.axis_index(axis)
    got = None
    for bit in bits_of(lax.axis_size(axis)):
        if got is not None:
            x = x + got
        x = x.reshape((x.shape[0] // 2, 2) + x.shape[1:])
        mine = (index // bit) % 2
        send = lax.dynamic_index_in_dim(x, 1 - mine, 1, keepdims=False)
        x = lax.dynamic_index_in_dim(x, mine, 1, keepdims=False)
        got = swap(send, axis, bit)
    return (x + got)[0]


def exchange(x, axis):
    size = lax.axis_size(axis)
    index = lax.axis_index(axis)
    sent = [lax.dynamic_index_in_dim(x, index ^ k, 0, keepdims=False) for k in range(size)]
    sent = lax.optimization_barrier(tuple(sent))
    got = [sent[0]] + [swap(sent[k], axis, k) for k in range(1, size)]
    return absolute(lax.optimization_barrier(tuple(got)), index)


def chain(front, structure, factor_front, factor_border, pivot_inverse):
    rows = lax.axis_size("row")
    cols = lax.axis_size("col")
    row_index = lax.axis_index("row")
    col_index = lax.axis_index("col")
    rows_here, cols_here = front.shape
    supers, width_here, width = pivot_inverse.shape
    fine = width_here // cols
    ratio = cols // rows
    part_cols = cols_here // HALVES
    row_flags = local_flags(structure, row_index, rows_here)
    col_flags = local_flags(structure, col_index, cols_here)

    own = [factor_front[k].T * row_flags[k][None, :] for k in range(supers)]
    factors = []
    for k in range(supers):
        if k == 0:
            pieces = quick(own[k], "col")
        else:
            even, odd = direct(own[k][None], "col", 0)
            pieces = [(even, odd)[j % 2][j // 2] for j in range(cols)]
        factors.append(absolute(pieces, col_index).reshape(width, rows_here))

    fronts = []
    partial_prev = None
    for k in range(supers):
        part = contract(factors[k], front, 1, 0)
        if k > 0:
            part = part - contract(factor_border[k - 1], partial_prev, 0, 0)
        partial_prev = part
        parts = []
        for h in range(HALVES):
            x = part[:, h * part_cols : (h + 1) * part_cols].reshape(rows, width_here, part_cols)
            x = scatter_sum(x, "row")
            parts.append(-(x * col_flags[k][None, h * part_cols : (h + 1) * part_cols]))
        fronts.append(jnp.concatenate(parts, axis=1))

    products = []
    for k in range(supers):
        spread = exchange(fronts[k].reshape(cols, fine, cols_here), "col")
        spread = spread.reshape(rows, ratio, fine, cols_here)
        lines = exchange(spread, "row")
        lines = jnp.swapaxes(lines, 1, 2).reshape(rows * fine, rows_here)
        products.append([contract(lines, f, 1, 1) for f in factors[k : k + 2]])
    grams = {}
    for members in (range(supers - 1), range(supers - 1, supers)):
        keys = [(k, k + j) for k in members for j in range(len(products[k]))]
        got = jnp.stack([products[k][m - k] for k, m in keys], axis=1)
        got = scatter_sum(got.reshape(rows, fine, len(keys), width), "row")
        got = relay(got, "col").reshape(width_here, len(keys), width)
        grams.update({key: got[:, i] for i, key in enumerate(keys)})

    parents = []
    diagonals = []
    for k in range(supers):
        diag = pivot_inverse[k] - grams[k, k]
        if k > 0:
            border = factor_border[k - 1]
            parent = grams[k - 1, k] + contract(diagonals[k - 1], border, 1, 0)
            parents.append(-parent)
            slots = jnp.swapaxes(parent.reshape(width_here, rows, width_here), 0, 1)
            sliver = exchange(slots, "row").reshape(width, width_here)
            diag = diag + contract(sliver, border, 0, 0)
        diagonals.append(diag)
    return (jnp.stack(fronts), jnp.stack(parents), jnp.stack(diagonals))


def solution(mesh):
    placed = (P("row", "col"), P(), P(None, "row", "col"), P(), P(None, "row", None))
    return jax.shard_map(
        chain,
        mesh=mesh,
        in_specs=placed,
        out_specs=(P(None, "row", "col"), P(None, "row", None), P(None, "row", None)),
        check_vma=False,
    )
```

time: 809 us -> 586 us (0.72)
  waiting for transfers between devices: 592 us -> 319 us
  starting transfers between devices: 1.37 us -> 91 us
  matrix products: 154 us -> 101 us
  other arithmetic: 29.1 us -> 42.2 us
  local copies, waits for them, and re-layouts: 12.1 us -> 24.5 us
  between operations: 14.6 us -> 2.37 us
    psum x2 -> x0, waiting for transfers between devices: 380 us -> none  [the longest x1 321 us: broadcast(): return lax.psum(jnp.where(mine, x, jnp.zeros_like(x)), axis)]
    ppermute x0 -> x74, waiting for transfers between devices: none -> 319 us  [swap(): return lax.ppermute(x, axis, [(i, i ^ bit) for i in range(size)])]
    all_gather x5 -> x0, waiting for transfers between devices: 125 us -> none  [the longest x3 79 us: body(): gathered = lax.all_gather(factor_front[section], 'col', axis=1, tiled=True)]
    ppermute x0 -> x74, starting transfers between devices: none -> 91 us  [swap(): return lax.ppermute(x, axis, [(i, i ^ bit) for i in range(size)])]
    reduce_scatter x3 -> x0, waiting for transfers between devices: 85.7 us -> none  [body(): lax.psum_scatter(partial_value, 'row', scatter_dimension=0, tiled=True)]
    dot_general x20 -> x14, matrix products: 154 us -> 101 us  [contract(): lax.dot_general(former, latter, (((former_dim,), (latter_dim,)), ((), ())...]
    concatenate x0 -> x16, other arithmetic: none -> 9.58 us  [the longest x2 6.24 us: direct(): even = jnp.concatenate(even, axis=join)]
    mul x3 -> x1, other arithmetic: 10.2 us -> 1.85 us  [chain(): own = [factor_front[k].T * row_flags[k][None, :] for k in range(supers)]]
  transfers between devices with their start and end apart: 10 -> 74, of which waited for: 10 -> 37; matrix products, arithmetic and copies ran while one was open for 21% -> 18% of each run, Pallas kernels for 0% -> 0%
where the time goes in v1:
time: 586 us; the launch traced here: 579 us
  waiting for transfers between devices  319 us (54%)
  matrix products  101 us (17%)
  starting transfers between devices  91 us (16%)
  other arithmetic  42.2 us (7%)
  local copies, waits for them, and re-layouts  24.5 us (4%)
    ppermute x74, waiting for transfers between devices, swap(): return lax.ppermute(x, axis, [(i, i ^ bit) for i in range(size)])  319 us
    dot_general x14, matrix products, contract(): lax.dot_general(former, latter, (((former_dim,), (latter_dim,)), ((), ())...  101 us
    ppermute x74, starting transfers between devices, swap(): return lax.ppermute(x, axis, [(i, i ^ bit) for i in range(size)])  91 us
    select_n x51, other arithmetic, absolute(): jnp.where(mine, h, l)  15.8 us
  transfers between devices with their start and end apart: 74, of which 37 were waited for; matrix products, arithmetic and copies ran while one was open for 18% of the time, Pallas kernels for 0%

profile of v1, /device:TPU:0, one launch (start us, length us, event | category | flops | bytes accessed | tf_op | source)
XLA Modules:
  0.0 579.3 jit_solution(4257123566033206650)
XLA Ops:
  11.0 14.1 %collective-permute-done.2 = f32[64,3072]{1,0:T(8,128)} collective-permute-done((f32[64,3072]{1,0:T(8,128)S(1)}, f32[64,3072]{1,0:T(8,128)}, u32[]{:S(2)}, u32[]{:S(2)}) %collective-permute-start.2) | collective-permute-done | bytes 786464 | tf_op jit(solution)/shard_map/ppermute | solution.py:25
  28.2 15.6 %collective-permute-done = f32[64,3072]{1,0:T(8,128)S(1)} collective-permute-done((f32[64,3072]{1,0:T(8,128)S(1)}, f32[64,3072]{1,0:T(8,128)S(1)}, u32[]{:S(2)}, u32[]{:S(2)}) %collective-permute-start) | collective-permute-done | bytes 786464 | tf_op jit(solution)/shard_map/ppermute | solution.py:25
  45.3 7.0 %collective-permute-done.1 = f32[32,3072]{1,0:T(8,128)S(1)} collective-permute-done((f32[32,3072]{1,0:T(8,128)S(1)}, f32[32,3072]{1,0:T(8,128)S(1)}, u32[]{:S(2)}, u32[]{:S(2)}) %collective-permute-start.1) | collective-permute-done | bytes 393248 | tf_op jit(solution)/shard_map/ppermute | solution.py:25
  55.4 29.8 %collective-permute-done.3 = f32[32,3072]{1,0:T(8,128)S(1)} collective-permute-done((f32[32,3072]{1,0:T(8,128)S(1)}, f32[32,3072]{1,0:T(8,128)S(1)}, u32[]{:S(2)}, u32[]{:S(2)}) %collective-permute-start.3) | collective-permute-done | bytes 393248 | tf_op jit(solution)/shard_map/ppermute | solution.py:25
  90.7 20.8 %fusion.128 = f32[512,1536]{1,0:T(8,128)S(1)} fusion(f32[512,3072]{1,0:T(8,128)S(1)} %bitcast.444, f32[3072,1536]{1,0:T(8,128)} %param.5), kind=kOutput, calls=%fused_computation.433 | convolution fusion | flops 14495514624 | bytes 28311552 | tf_op jit(solution)/shard_map/dot_general | solution.py:14
  116.5 17.2 %collective-permute-done.8 = f32[2,128,768]{2,1,0:T(8,128)S(1)} collective-permute-done((f32[2,128,768]{2,1,0:T(8,128)S(1)}, f32[2,128,768]{2,1,0:T(8,128)S(1)}, u32[]{:S(2)}, u32[]{:S(2)}) %collective-permute-start.8) | collective-permute-done | bytes 786464 | tf_op jit(solution)/shard_map/ppermute | solution.py:25
  138.8 19.5 %collective-permute-done.10 = f32[2,128,768]{2,1,0:T(8,128)} collective-permute-done((f32[2,128,768]{2,1,0:T(8,128)}, f32[2,128,768]{2,1,0:T(8,128)}, u32[]{:S(2)}, u32[]{:S(2)}) %collective-permute-start.10) | collective-permute-done | bytes 786464 | tf_op jit(solution)/shard_map/ppermute | solution.py:25
  163.0 17.5 %collective-permute-done.11 = f32[1,128,768]{2,1,0:T(8,128)S(1)} collective-permute-done((f32[1,128,768]{2,1,0:T(8,128)S(1)}, f32[1,128,768]{2,1,0:T(8,128)S(1)}, u32[]{:S(2)}, u32[]{:S(2)}) %collective-permute-start.11) | collective-permute-done | bytes 393248 | tf_op jit(solution)/shard_map/ppermute | solution.py:25
  182.9 18.0 %collective-permute-done.12 = f32[1,64,3072]{2,1,0:T(8,128)S(1)} collective-permute-done((f32[1,64,3072]{2,1,0:T(8,128)S(1)}, f32[1,64,3072]{2,1,0:T(8,128)S(1)}, u32[]{:S(2)}, u32[]{:S(2)}) %collective-permute-start.12) | collective-permute-done | bytes 786464 | tf_op jit(solution)/shard_map/ppermute | solution.py:25
  205.0 12.8 %collective-permute-done.20 = f32[1,64,3072]{2,1,0:T(8,128)S(1)} collective-permute-done((f32[1,64,3072]{2,1,0:T(8,128)S(1)}, f32[1,64,3072]{2,1,0:T(8,128)S(1)}, u32[]{:S(2)}, u32[]{:S(2)}) %collective-permute-start.20) | collective-permute-done | bytes 786464 | tf_op jit(solution)/shard_map/ppermute | solution.py:25
  231.6 5.3 collective-permute-done.35
  236.9 6.9 %collective-permute-done.36 = f32[2,16,1536]{2,1,0:T(8,128)S(1)} collective-permute-done((f32[2,16,1536]{2,1,0:T(8,128)S(1)}, f32[2,16,1536]{2,1,0:T(8,128)S(1)}, u32[]{:S(2)}, u32[]{:S(2)}) %collective-permute-start.36) | collective-permute-done | bytes 196640 | tf_op jit(solution)/shard_map/ppermute | solution.py:25
  247.3 5.8 %convolution_bitcast_fusion.5 = f32[2,2,16,1,512]{4,2,1,0,3:T(8,128)S(1)} fusion(f32[2,2,16,3072]{3,2,1,0:T(8,128)S(1)} %dot_general.67, f32[512,3072,1,1]{1,0,3,2:T(8,128)} %bitcast.445), kind=kOutput, calls=%fused_computation.100 | convolution fusion | flops 603979776 | bytes 7208960 | tf_op jit(solution)/shard_map/dot_general | solution.py:14
  258.2 21.0 %fusion.130 = f32[512,1536]{1,0:T(8,128)S(1)} fusion(f32[512,3072]{1,0:T(8,128)S(1)} %bitcast.438, f32[3072,1536]{1,0:T(8,128)} %param.5), kind=kOutput, calls=%fused_computation.435 | convolution fusion | flops 14495514624 | bytes 28311552 | tf_op jit(solution)/shard_map/dot_general | solution.py:14
  284.0 21.1 %fusion.129 = f32[512,1536]{1,0:T(8,128)S(1)} fusion(f32[512,3072]{1,0:T(8,128)S(1)} %bitcast.441, f32[3072,1536]{1,0:T(8,128)} %param.5), kind=kOutput, calls=%fused_computation.434 | convolution fusion | flops 14495514624 | bytes 28311552 | tf_op jit(solution)/shard_map/dot_general | solution.py:14
  311.3 3.9 collective-permute-start.16
  320.9 12.7 %collective-permute-done.16 = f32[2,128,768]{2,1,0:T(8,128)S(1)} collective-permute-done((f32[2,128,768]{2,1,0:T(8,128)S(1)}, f32[2,128,768]{2,1,0:T(8,128)S(1)}, u32[]{:S(2)}, u32[]{:S(2)}) %collective-permute-start.16) | collective-permute-done | bytes 786464 | tf_op jit(solution)/shard_map/ppermute | solution.py:25
  336.8 22.1 %collective-permute-done.18 = f32[2,128,768]{2,1,0:T(8,128)S(1)} collective-permute-done((f32[2,128,768]{2,1,0:T(8,128)S(1)}, f32[2,128,768]{2,1,0:T(8,128)S(1)}, u32[]{:S(2)}, u32[]{:S(2)}) %collective-permute-start.18) | collective-permute-done | bytes 786464 | tf_op jit(solution)/shard_map/ppermute | solution.py:25
  359.6 24.6 %collective-permute-done.24 = f32[2,128,768]{2,1,0:T(8,128)S(1)} collective-permute-done((f32[2,128,768]{2,1,0:T(8,128)S(1)}, f32[2,128,768]{2,1,0:T(8,128)S(1)}, u32[]{:S(2)}, u32[]{:S(2)}) %collective-permute-start.24) | collective-permute-done | bytes 786464 | tf_op jit(solution)/shard_map/ppermute | solution.py:25
  384.9 15.6 %collective-permute-done.26 = f32[2,128,768]{2,1,0:T(8,128)S(1)} collective-permute-done((f32[2,128,768]{2,1,0:T(8,128)S(1)}, f32[2,128,768]{2,1,0:T(8,128)S(1)}, u32[]{:S(2)}, u32[]{:S(2)}) %collective-permute-start.26) | collective-permute-done | bytes 786464 | tf_op jit(solution)/shard_map/ppermute | solution.py:25
  402.9 24.1 %collective-permute-done.25 = f32[1,128,768]{2,1,0:T(8,128)S(1)} collective-permute-done((f32[1,128,768]{2,1,0:T(8,128)S(1)}, f32[1,128,768]{2,1,0:T(8,128)S(1)}, u32[]{:S(2)}, u32[]{:S(2)}) %collective-permute-start.25) | collective-permute-done | bytes 393248 | tf_op jit(solution)/shard_map/ppermute | solution.py:25
  428.9 5.8 collective-permute-done.27
  451.9 3.5 collective-permute-done.60
  462.6 3.5 collective-permute-done.46
  469.6 5.8 convolution_bitcast_fusion.3
  475.3 6.4 %convolution_bitcast_fusion.2 = f32[2,2,16,1,512]{4,2,1,0,3:T(8,128)} fusion(f32[2,2,16,3072]{3,2,1,0:T(8,128)S(1)} %dot_general.72, f32[512,3072,1,1]{1,0,3,2:T(8,128)} %bitcast.439), kind=kOutput, calls=%fused_computation.97 | convolution fusion | flops 603979776 | bytes 7208960 | tf_op jit(solution)/shard_map/dot_general | solution.py:14
  488.5 5.8 %fusion.131 = f32[2,2,16,512]{3,2,1,0:T(8,128)S(1)} fusion(f32[2,2,16,3072]{3,2,1,0:T(8,128)S(1)} %dot_general.80, f32[512,3072,1,1]{1,0,3,2:T(8,128)} %bitcast.440), kind=kOutput, calls=%fused_computation.436 | convolution fusion | flops 603979776 | bytes 7208960 | tf_op jit(solution)/shard_map/dot_general | solution.py:14
  494.3 12.0 %collective-permute-start.66 = (f32[2,16,1,512]{3,1,0,2:T(8,128)S(1)}, f32[2,16,1,512]{3,1,0,2:T(8,128)S(1)}, u32[]{:S(2)}, u32[]{:S(2)}) collective-permute-start(f32[2,16,1,512]{3,1,0,2:T(8,128)S(1)} %dynamic-slice_bitcast_fusion.19), channel_id=1, source_target_pairs={{0,8},{8,0},{16,24},{24,16},{1,9},{9,1},{17,25},{25,17},{2,10},{10... | collective-permute-start | bytes 196616 | tf_op jit(solution)/shard_map/ppermute | solution.py:25
  508.9 3.6 collective-permute-start.67
  517.4 6.5 %collective-permute-done.49 = f32[1,16,4,512]{3,1,0,2:T(8,128)S(1)} collective-permute-done((f32[1,16,4,512]{3,1,0,2:T(8,128)S(1)}, f32[1,16,4,512]{3,1,0,2:T(8,128)S(1)}, u32[]{:S(2)}, u32[]{:S(2)}) %collective-permute-start.49) | collective-permute-done | bytes 131104 | tf_op jit(solution)/shard_map/ppermute | solution.py:25
  529.1 5.1 collective-permute-done.51
  536.7 11.1 %collective-permute-done.52 = f32[4,16,4,512]{3,1,0,2:T(8,128)S(1)} collective-permute-done((f32[4,16,4,512]{3,1,0,2:T(8,128)S(1)}, f32[4,16,4,512]{3,1,0,2:T(8,128)S(1)}, u32[]{:S(2)}, u32[]{:S(2)}) %collective-permute-start.52) | collective-permute-done | bytes 524320 | tf_op jit(solution)/shard_map/ppermute | solution.py:25
  (341 shorter events, 172.4 us)
Async XLA Ops:
  3.5 40.5 %collective-permute-start.7 = (f32[64,3072]{1,0:T(8,128)S(1)}, f32[64,3072]{1,0:T(8,128)}, u32[]{:S(2)}, u32[]{:S(2)}) collective-permute-start(f32[64,3072]{1,0:T(8,128)S(1)} %get-tuple-element.243), channel_id=1, source_target_pairs={{0,1},{1,0},{2,3},{3,2},{4,5},{5,4},{6,7},{7,6},{8,9},{9,8},{10,11... | collective-permute-start | bytes 2359304 | tf_op jit(solution)/shard_map/ppermute | solution.py:25
  4.0 21.1 %collective-permute-start.2 = (f32[64,3072]{1,0:T(8,128)S(1)}, f32[64,3072]{1,0:T(8,128)}, u32[]{:S(2)}, u32[]{:S(2)}) collective-permute-start(f32[64,3072]{1,0:T(8,128)S(1)} %get-tuple-element.243), channel_id=1, source_target_pairs={{0,2},{1,3},{2,0},{3,1},{4,6},{5,7},{6,4},{7,5},{8,10},{9,11},{10,... | collective-permute-start | bytes 2359304 | tf_op jit(solution)/shard_map/ppermute | solution.py:25
  6.6 37.3 %collective-permute-start = (f32[64,3072]{1,0:T(8,128)S(1)}, f32[64,3072]{1,0:T(8,128)S(1)}, u32[]{:S(2)}, u32[]{:S(2)}) collective-permute-start(f32[64,3072]{1,0:T(8,128)S(1)} %get-tuple-element.243), channel_id=1, source_target_pairs={{0,4},{1,5},{2,6},{3,7},{4,0},{5,1},{6,2},{7,3},{8,12},{9,13},{10,... | collective-permute-start | bytes 2359304 | tf_op jit(solution)/shard_map/ppermute | solution.py:25
  8.1 196.3 %collective-permute-start.22 = (f32[1,64,3072]{2,1,0:T(8,128)S(1)}, f32[1,64,3072]{2,1,0:T(8,128)}, u32[]{:S(2)}, u32[]{:S(2)}) collective-permute-start(f32[1,64,3072]{2,1,0:T(8,128)S(1)} %get-tuple-element.244), channel_id=1, source_target_pairs={{0,6},{1,7},{2,4},{3,5},{4,2},{5,3},{6,0},{7,1},{8,14},{9,15},{10,... | collective-permute-start | bytes 2359304 | tf_op jit(solution)/shard_map/ppermute | solution.py:25
  8.1 196.4 %collective-permute-start.21 = (f32[1,64,3072]{2,1,0:T(8,128)S(1)}, f32[1,64,3072]{2,1,0:T(8,128)}, u32[]{:S(2)}, u32[]{:S(2)}) collective-permute-start(f32[1,64,3072]{2,1,0:T(8,128)S(1)} %get-tuple-element.244), channel_id=1, source_target_pairs={{0,4},{1,5},{2,6},{3,7},{4,0},{5,1},{6,2},{7,3},{8,12},{9,13},{10,... | collective-permute-start | bytes 2359304 | tf_op jit(solution)/shard_map/ppermute | solution.py:25
  26.1 59.1 %collective-permute-start.3 = (f32[32,3072]{1,0:T(8,128)S(1)}, f32[32,3072]{1,0:T(8,128)S(1)}, u32[]{:S(2)}, u32[]{:S(2)}) collective-permute-start(f32[32,3072]{1,0:T(8,128)S(1)} %slice.220), channel_id=1, source_target_pairs={{0,4},{1,5},{2,6},{3,7},{4,0},{5,1},{6,2},{7,3},{8,12},{9,13},{10,... | collective-permute-start | bytes 1179656 | tf_op jit(solution)/shard_map/ppermute | solution.py:25
  44.0 41.2 %collective-permute-start.6 = (f32[64,3072]{1,0:T(8,128)}, f32[64,3072]{1,0:T(8,128)S(1)}, u32[]{:S(2)}, u32[]{:S(2)}) collective-permute-start(f32[64,3072]{1,0:T(8,128)} %collective-permute-done.2), channel_id=1, source_target_pairs={{0,1},{1,0},{2,3},{3,2},{4,5},{5,4},{6,7},{7,6},{8,9},{9,8},{10,11... | collective-permute-start | bytes 2359304 | tf_op jit(solution)/shard_map/ppermute | solution.py:25
  52.3 128.8 %collective-permute-start.14 = (f32[1,64,3072]{2,1,0:T(8,128)S(1)}, f32[1,64,3072]{2,1,0:T(8,128)}, u32[]{:S(2)}, u32[]{:S(2)}) collective-permute-start(f32[1,64,3072]{2,1,0:T(8,128)S(1)} %get-tuple-element.245), channel_id=1, source_target_pairs={{0,6},{1,7},{2,4},{3,5},{4,2},{5,3},{6,0},{7,1},{8,14},{9,15},{10,... | collective-permute-start | bytes 2359304 | tf_op jit(solution)/shard_map/ppermute | solution.py:25
  113.3 20.5 %collective-permute-start.8 = (f32[2,128,768]{2,1,0:T(8,128)S(1)}, f32[2,128,768]{2,1,0:T(8,128)S(1)}, u32[]{:S(2)}, u32[]{:S(2)}) collective-permute-start(f32[2,128,768]{2,1,0:T(8,128)S(1)} %dynamic-slice_bitcast_fusion.5), channel_id=1, source_target_pairs={{0,8},{8,0},{16,24},{24,16},{1,9},{9,1},{17,25},{25,17},{2,10},{10... | collective-permute-start | bytes 2359304 | tf_op jit(solution)/shard_map/ppermute | solution.py:25
  116.0 42.3 %collective-permute-start.10 = (f32[2,128,768]{2,1,0:T(8,128)}, f32[2,128,768]{2,1,0:T(8,128)}, u32[]{:S(2)}, u32[]{:S(2)}) collective-permute-start(f32[2,128,768]{2,1,0:T(8,128)} %dynamic-slice_bitcast_fusion.4), channel_id=1, source_target_pairs={{0,8},{8,0},{16,24},{24,16},{1,9},{9,1},{17,25},{25,17},{2,10},{10... | collective-permute-start | bytes 2359304 | tf_op jit(solution)/shard_map/ppermute | solution.py:25
  135.5 25.5 %collective-permute-start.9 = (f32[1,128,768]{2,1,0:T(8,128)}, f32[1,128,768]{2,1,0:T(8,128)S(1)}, u32[]{:S(2)}, u32[]{:S(2)}) collective-permute-start(f32[1,128,768]{2,1,0:T(8,128)} %constant_dynamic-slice_fusion.16), channel_id=1, source_target_pairs={{0,16},{8,24},{16,0},{24,8},{1,17},{9,25},{17,1},{25,9},{2,18},{10... | collective-permute-start | bytes 1179656 | tf_op jit(solution)/shard_map/ppermute | solution.py:25
  158.3 24.5 %collective-permute-start.13 = (f32[1,64,3072]{2,1,0:T(8,128)S(1)}, f32[1,64,3072]{2,1,0:T(8,128)S(1)}, u32[]{:S(2)}, u32[]{:S(2)}) collective-permute-start(f32[1,64,3072]{2,1,0:T(8,128)S(1)} %get-tuple-element.245), channel_id=1, source_target_pairs={{0,4},{1,5},{2,6},{3,7},{4,0},{5,1},{6,2},{7,3},{8,12},{9,13},{10,... | collective-permute-start | bytes 2359304 | tf_op jit(solution)/shard_map/ppermute | solution.py:25
  180.5 20.4 %collective-permute-start.12 = (f32[1,64,3072]{2,1,0:T(8,128)S(1)}, f32[1,64,3072]{2,1,0:T(8,128)S(1)}, u32[]{:S(2)}, u32[]{:S(2)}) collective-permute-start(f32[1,64,3072]{2,1,0:T(8,128)S(1)} %get-tuple-element.245), channel_id=1, source_target_pairs={{0,2},{1,3},{2,0},{3,1},{4,6},{5,7},{6,4},{7,5},{8,10},{9,11},{10,... | collective-permute-start | bytes 2359304 | tf_op jit(solution)/shard_map/ppermute | solution.py:25
  181.2 36.6 %collective-permute-start.20 = (f32[1,64,3072]{2,1,0:T(8,128)S(1)}, f32[1,64,3072]{2,1,0:T(8,128)S(1)}, u32[]{:S(2)}, u32[]{:S(2)}) collective-permute-start(f32[1,64,3072]{2,1,0:T(8,128)S(1)} %get-tuple-element.244), channel_id=1, source_target_pairs={{0,2},{1,3},{2,0},{3,1},{4,6},{5,7},{6,4},{7,5},{8,10},{9,11},{10,... | collective-permute-start | bytes 2359304 | tf_op jit(solution)/shard_map/ppermute | solution.py:25
  182.8 34.9 %collective-permute-start.28 = (f32[16,1536]{1,0:T(8,128)S(1)}, f32[16,1536]{1,0:T(8,128)S(1)}, u32[]{:S(2)}, u32[]{:S(2)}) collective-permute-start(f32[16,1536]{1,0:T(8,128)S(1)} %get-tuple-element.92), channel_id=1, source_target_pairs={{0,1},{1,0},{2,3},{3,2},{4,5},{5,4},{6,7},{7,6},{8,9},{9,8},{10,11... | collective-permute-start | bytes 294920 | tf_op jit(solution)/shard_map/ppermute | solution.py:25
  204.5 19.6 %collective-permute-start.31 = (f32[16,1536]{1,0:T(8,128)S(1)}, f32[16,1536]{1,0:T(8,128)S(1)}, u32[]{:S(2)}, u32[]{:S(2)}) collective-permute-start(f32[16,1536]{1,0:T(8,128)S(1)} %get-tuple-element.95), channel_id=1, source_target_pairs={{0,4},{1,5},{2,6},{3,7},{4,0},{5,1},{6,2},{7,3},{8,12},{9,13},{10,... | collective-permute-start | bytes 294920 | tf_op jit(solution)/shard_map/ppermute | solution.py:25
  223.9 29.2 %collective-permute-start.23 = (f32[4,64,3072]{2,1,0:T(8,128)}, f32[4,64,3072]{2,1,0:T(8,128)}, u32[]{:S(2)}, u32[]{:S(2)}) collective-permute-start(f32[4,64,3072]{2,1,0:T(8,128)} %pad_maximum_fusion.8), channel_id=1, source_target_pairs={{0,1},{1,0},{2,3},{3,2},{4,5},{5,4},{6,7},{7,6},{8,9},{9,8},{10,11... | collective-permute-start | bytes 9437192 | tf_op jit(solution)/shard_map/ppermute | solution.py:25
  224.2 55.0 %collective-permute-start.15 = (f32[4,64,3072]{2,1,0:T(8,128)}, f32[4,64,3072]{2,1,0:T(8,128)}, u32[]{:S(2)}, u32[]{:S(2)}) collective-permute-start(f32[4,64,3072]{2,1,0:T(8,128)} %pad_maximum_fusion.5), channel_id=1, source_target_pairs={{0,1},{1,0},{2,3},{3,2},{4,5},{5,4},{6,7},{7,6},{8,9},{9,8},{10,11... | collective-permute-start | bytes 9437192 | tf_op jit(solution)/shard_map/ppermute | solution.py:25
  311.3 22.3 %collective-permute-start.16 = (f32[2,128,768]{2,1,0:T(8,128)S(1)}, f32[2,128,768]{2,1,0:T(8,128)S(1)}, u32[]{:S(2)}, u32[]{:S(2)}) collective-permute-start(f32[2,128,768]{2,1,0:T(8,128)S(1)} %dynamic-slice_bitcast_fusion.3), channel_id=1, source_target_pairs={{0,8},{8,0},{16,24},{24,16},{1,9},{9,1},{17,25},{25,17},{2,10},{10... | collective-permute-start | bytes 2359304 | tf_op jit(solution)/shard_map/ppermute | solution.py:25
  315.5 43.4 %collective-permute-start.18 = (f32[2,128,768]{2,1,0:T(8,128)S(1)}, f32[2,128,768]{2,1,0:T(8,128)S(1)}, u32[]{:S(2)}, u32[]{:S(2)}) collective-permute-start(f32[2,128,768]{2,1,0:T(8,128)S(1)} %dynamic-slice_bitcast_fusion.2), channel_id=1, source_target_pairs={{0,8},{8,0},{16,24},{24,16},{1,9},{9,1},{17,25},{25,17},{2,10},{10... | collective-permute-start | bytes 2359304 | tf_op jit(solution)/shard_map/ppermute | solution.py:25
  315.7 68.5 %collective-permute-start.24 = (f32[2,128,768]{2,1,0:T(8,128)S(1)}, f32[2,128,768]{2,1,0:T(8,128)S(1)}, u32[]{:S(2)}, u32[]{:S(2)}) collective-permute-start(f32[2,128,768]{2,1,0:T(8,128)S(1)} %dynamic-slice_bitcast_fusion.1), channel_id=1, source_target_pairs={{0,8},{8,0},{16,24},{24,16},{1,9},{9,1},{17,25},{25,17},{2,10},{10... | collective-permute-start | bytes 2359304 | tf_op jit(solution)/shard_map/ppermute | solution.py:25
  320.8 79.6 %collective-permute-start.26 = (f32[2,128,768]{2,1,0:T(8,128)S(1)}, f32[2,128,768]{2,1,0:T(8,128)S(1)}, u32[]{:S(2)}, u32[]{:S(2)}) collective-permute-start(f32[2,128,768]{2,1,0:T(8,128)S(1)} %dynamic-slice_bitcast_fusion), channel_id=1, source_target_pairs={{0,8},{8,0},{16,24},{24,16},{1,9},{9,1},{17,25},{25,17},{2,10},{10... | collective-permute-start | bytes 2359304 | tf_op jit(solution)/shard_map/ppermute | solution.py:25
  333.8 66.9 %collective-permute-start.17 = (f32[1,128,768]{2,1,0:T(8,128)S(1)}, f32[1,128,768]{2,1,0:T(8,128)S(1)}, u32[]{:S(2)}, u32[]{:S(2)}) collective-permute-start(f32[1,128,768]{2,1,0:T(8,128)S(1)} %constant_dynamic-slice_fusion.13), channel_id=1, source_target_pairs={{0,16},{8,24},{16,0},{24,8},{1,17},{9,25},{17,1},{25,9},{2,18},{10... | collective-permute-start | bytes 1179656 | tf_op jit(solution)/shard_map/ppermute | solution.py:25
  359.0 41.8 %collective-permute-start.19 = (f32[1,128,768]{2,1,0:T(8,128)S(1)}, f32[1,128,768]{2,1,0:T(8,128)S(1)}, u32[]{:S(2)}, u32[]{:S(2)}) collective-permute-start(f32[1,128,768]{2,1,0:T(8,128)S(1)} %constant_dynamic-slice_fusion.12), channel_id=1, source_target_pairs={{0,16},{8,24},{16,0},{24,8},{1,17},{9,25},{17,1},{25,9},{2,18},{10... | collective-permute-start | bytes 1179656 | tf_op jit(solution)/shard_map/ppermute | solution.py:25
  384.3 42.8 %collective-permute-start.25 = (f32[1,128,768]{2,1,0:T(8,128)S(1)}, f32[1,128,768]{2,1,0:T(8,128)S(1)}, u32[]{:S(2)}, u32[]{:S(2)}) collective-permute-start(f32[1,128,768]{2,1,0:T(8,128)S(1)} %constant_dynamic-slice_fusion.11), channel_id=1, source_target_pairs={{0,16},{8,24},{16,0},{24,8},{1,17},{9,25},{17,1},{25,9},{2,18},{10... | collective-permute-start | bytes 1179656 | tf_op jit(solution)/shard_map/ppermute | solution.py:25
  400.6 34.0 %collective-permute-start.27 = (f32[1,128,768]{2,1,0:T(8,128)S(1)}, f32[1,128,768]{2,1,0:T(8,128)S(1)}, u32[]{:S(2)}, u32[]{:S(2)}) collective-permute-start(f32[1,128,768]{2,1,0:T(8,128)S(1)} %constant_dynamic-slice_fusion.10), channel_id=1, source_target_pairs={{0,16},{8,24},{16,0},{24,8},{1,17},{9,25},{17,1},{25,9},{2,18},{10... | collective-permute-start | bytes 1179656 | tf_op jit(solution)/shard_map/ppermute | solution.py:25
  401.0 36.3 %collective-permute-start.38 = (f32[16,1536]{1,0:T(8,128)S(1)}, f32[16,1536]{1,0:T(8,128)S(1)}, u32[]{:S(2)}, u32[]{:S(2)}) collective-permute-start(f32[16,1536]{1,0:T(8,128)S(1)} %get-tuple-element.116), channel_id=1, source_target_pairs={{0,1},{1,0},{2,3},{3,2},{4,5},{5,4},{6,7},{7,6},{8,9},{9,8},{10,11... | collective-permute-start | bytes 294920 | tf_op jit(solution)/shard_map/ppermute | solution.py:25
  401.1 37.7 %collective-permute-start.39 = (f32[16,1536]{1,0:T(8,128)S(1)}, f32[16,1536]{1,0:T(8,128)S(1)}, u32[]{:S(2)}, u32[]{:S(2)}) collective-permute-start(f32[16,1536]{1,0:T(8,128)S(1)} %get-tuple-element.117), channel_id=1, source_target_pairs={{0,2},{1,3},{2,0},{3,1},{4,6},{5,7},{6,4},{7,5},{8,10},{9,11},{10,... | collective-permute-start | bytes 294920 | tf_op jit(solution)/shard_map/ppermute | solution.py:25
  401.8 39.1 %collective-permute-start.40 = (f32[16,1536]{1,0:T(8,128)S(1)}, f32[16,1536]{1,0:T(8,128)S(1)}, u32[]{:S(2)}, u32[]{:S(2)}) collective-permute-start(f32[16,1536]{1,0:T(8,128)S(1)} %get-tuple-element.118), channel_id=1, source_target_pairs={{0,3},{1,2},{2,1},{3,0},{4,7},{5,6},{6,5},{7,4},{8,11},{9,10},{10,... | collective-permute-start | bytes 294920 | tf_op jit(solution)/shard_map/ppermute | solution.py:25
  458.2 23.6 %collective-permute-start.63 = (f32[2,16,1536]{2,1,0:T(8,128)}, f32[2,16,1536]{2,1,0:T(8,128)}, u32[]{:S(2)}, u32[]{:S(2)}) collective-permute-start(f32[2,16,1536]{2,1,0:T(8,128)} %get-tuple-element.164), channel_id=1, source_target_pairs={{0,8},{8,0},{16,24},{24,16},{1,9},{9,1},{17,25},{25,17},{2,10},{10... | collective-permute-start | bytes 589832 | tf_op jit(solution)/shard_map/ppermute | solution.py:25
  458.2 24.8 %collective-permute-start.64 = (f32[2,16,1536]{2,1,0:T(8,128)}, f32[2,16,1536]{2,1,0:T(8,128)}, u32[]{:S(2)}, u32[]{:S(2)}) collective-permute-start(f32[2,16,1536]{2,1,0:T(8,128)} %get-tuple-element.165), channel_id=1, source_target_pairs={{0,16},{8,24},{16,0},{24,8},{1,17},{9,25},{17,1},{25,9},{2,18},{10... | collective-permute-start | bytes 589832 | tf_op jit(solution)/shard_map/ppermute | solution.py:25
  461.1 21.8 %collective-permute-start.65 = (f32[2,16,1536]{2,1,0:T(8,128)}, f32[2,16,1536]{2,1,0:T(8,128)}, u32[]{:S(2)}, u32[]{:S(2)}) collective-permute-start(f32[2,16,1536]{2,1,0:T(8,128)} %get-tuple-element.166), channel_id=1, source_target_pairs={{0,24},{8,16},{16,8},{24,0},{1,25},{9,17},{17,9},{25,1},{2,26},{10... | collective-permute-start | bytes 589832 | tf_op jit(solution)/shard_map/ppermute | solution.py:25
  (66 other events, 809.8 us)

commit v2 on v1

--- a/solution.py
+++ b/solution.py
@@ -59,26 +59,23 @@
     return x
 
 
-def direct(x, axis, join):
+def direct(x, axis):
     size = lax.axis_size(axis)
-    even = [x] + [swap(x, axis, k) for k in range(2, size, 2)]
-    even = jnp.concatenate(even, axis=join)
-    return even, swap(even, axis, 1)
+    near = {k: swap(x, axis, k) if k else x for k in range(0, size, 2)}
+    near.update({k + 1: swap(near[k], axis, 1) for k in range(0, size, 2)})
+    return [near[k] for k in range(size)]
 
 
 def quick(x, axis):
     size = lax.axis_size(axis)
     if size != 8:
-        even, odd = direct(x[None], axis, 0)
-        return [(even, odd)[j % 2][j // 2] for j in range(size)]
+        return direct(x, axis)
     cut = x.shape[0] // 2
     near = {0: x}
     for k in (2, 4):
         near[k] = swap(x, axis, k)
     sides = {1: swap(x, axis, 1)}
-    near[6] = jnp.concatenate(
-        [swap(near[4][:cut], axis, 2), swap(near[2][cut:], axis, 4)], axis=0
-    )
+    near[6] = jnp.concatenate([swap(near[4][:cut], axis, 2), swap(near[2][cut:], axis, 4)], axis=0)
     for k in (2, 4, 6):
         sides[k + 1] = swap(near[k], axis, 1)
     near.update(sides)
@@ -127,8 +124,7 @@
         if k == 0:
             pieces = quick(own[k], "col")
         else:
-            even, odd = direct(own[k][None], "col", 0)
-            pieces = [(even, odd)[j % 2][j // 2] for j in range(cols)]
+            pieces = direct(own[k], "col")
         factors.append(absolute(pieces, col_index).reshape(width, rows_here))
 
     fronts = []
@@ -153,12 +149,12 @@
         lines = jnp.swapaxes(lines, 1, 2).reshape(rows * fine, rows_here)
         products.append([contract(lines, f, 1, 1) for f in factors[k : k + 2]])
     grams = {}
-    for members in (range(supers - 1), range(supers - 1, supers)):
-        keys = [(k, k + j) for k in members for j in range(len(products[k]))]
-        got = jnp.stack([products[k][m - k] for k, m in keys], axis=1)
-        got = scatter_sum(got.reshape(rows, fine, len(keys), width), "row")
-        got = relay(got, "col").reshape(width_here, len(keys), width)
-        grams.update({key: got[:, i] for i, key in enumerate(keys)})
+    for k in range(supers):
+        count = len(products[k])
+        got = jnp.stack(products[k], axis=1).reshape(rows, fine, count, width)
+        got = scatter_sum(got, "row")
+        got = relay(got, "col").reshape(width_here, count, width)
+        grams.update({(k, k + j): got[:, j] for j in range(count)})
 
     parents = []
     diagonals = []

time: 586 us -> 529 us (0.903)
  waiting for transfers between devices: 319 us -> 273 us
  starting transfers between devices: 91 us -> 101 us
  local copies, waits for them, and re-layouts: 24.5 us -> 15.4 us
  other arithmetic: 42.2 us -> 33.3 us
    ppermute x74 -> x85, waiting for transfers between devices: 319 us -> 273 us  [swap(): return lax.ppermute(x, axis, [(i, i ^ bit) for i in range(size)])]
    ppermute x74 -> x85, starting transfers between devices: 91 us -> 101 us  [swap(): return lax.ppermute(x, axis, [(i, i ^ bit) for i in range(size)])]
    another operation x8, other arithmetic: 9.87 us -> 3.58 us  [chain(): return (jnp.stack(fronts), jnp.stack(parents), jnp.stack(diagonals))]
    concatenate x2 -> x0, other arithmetic: 6.24 us -> none  [direct(): even = jnp.concatenate(even, axis=join)]
    select_n x51 -> x57, other arithmetic: 15.8 us -> 19.1 us  [absolute(): jnp.where(mine, h, l)]
  transfers between devices with their start and end apart: 74 -> 85, of which waited for: 37 -> 36; matrix products, arithmetic and copies ran while one was open for 18% -> 20% of each run, Pallas kernels for 0% -> 0%
where the time goes in v2:
time: 529 us; the launch traced here: 523 us
  waiting for transfers between devices  273 us (52%)
  starting transfers between devices  101 us (19%)
  matrix products  98.2 us (19%)
  other arithmetic  33.3 us (6%)
  local copies, waits for them, and re-layouts  15.4 us (3%)
    ppermute x85, waiting for transfers between devices, swap(): return lax.ppermute(x, axis, [(i, i ^ bit) for i in range(size)])  273 us
    ppermute x85, starting transfers between devices, swap(): return lax.ppermute(x, axis, [(i, i ^ bit) for i in range(size)])  101 us
    dot_general x14, matrix products, contract(): lax.dot_general(former, latter, (((former_dim,), (latter_dim,)), ((), ())...  98.2 us
    select_n x57, other arithmetic, absolute(): jnp.where(mine, h, l)  19.1 us
  transfers between devices with their start and end apart: 85, of which 36 were waited for; matrix products, arithmetic and copies ran while one was open for 20% of the time, Pallas kernels for 0%

profile of v2, /device:TPU:0, one launch (start us, length us, event | category | flops | bytes accessed | tf_op | source)
XLA Modules:
  0.0 523.2 jit_solution(12319284768888523116)
XLA Ops:
  10.7 14.3 %collective-permute-done.2 = f32[64,3072]{1,0:T(8,128)} collective-permute-done((f32[64,3072]{1,0:T(8,128)S(1)}, f32[64,3072]{1,0:T(8,128)}, u32[]{:S(2)}, u32[]{:S(2)}) %collective-permute-start.2) | collective-permute-done | bytes 786464 | tf_op jit(solution)/shard_map/ppermute | solution.py:25
  32.5 9.4 %collective-permute-done.27 = f32[64,3072]{1,0:T(8,128)} collective-permute-done((f32[64,3072]{1,0:T(8,128)S(1)}, f32[64,3072]{1,0:T(8,128)}, u32[]{:S(2)}, u32[]{:S(2)}) %collective-permute-start.27) | collective-permute-done | bytes 786464 | tf_op jit(solution)/shard_map/ppermute | solution.py:25
  44.1 22.8 %collective-permute-done.1 = f32[32,3072]{1,0:T(8,128)S(1)} collective-permute-done((f32[32,3072]{1,0:T(8,128)S(1)}, f32[32,3072]{1,0:T(8,128)S(1)}, u32[]{:S(2)}, u32[]{:S(2)}) %collective-permute-start.1) | collective-permute-done | bytes 393248 | tf_op jit(solution)/shard_map/ppermute | solution.py:25
  75.0 12.4 %collective-permute-done.16 = f32[64,3072]{1,0:T(8,128)} collective-permute-done((f32[64,3072]{1,0:T(8,128)S(1)}, f32[64,3072]{1,0:T(8,128)}, u32[]{:S(2)}, u32[]{:S(2)}) %collective-permute-start.16) | collective-permute-done | bytes 786464 | tf_op jit(solution)/shard_map/ppermute | solution.py:25
  87.4 17.0 %collective-permute-done.14 = f32[64,3072]{1,0:T(8,128)S(1)} collective-permute-done((f32[64,3072]{1,0:T(8,128)S(1)}, f32[64,3072]{1,0:T(8,128)S(1)}, u32[]{:S(2)}, u32[]{:S(2)}) %collective-permute-start.14) | collective-permute-done | bytes 786464 | tf_op jit(solution)/shard_map/ppermute | solution.py:25
  113.8 20.6 %fusion.139 = f32[512,1536]{1,0:T(8,128)S(1)} fusion(f32[512,3072]{1,0:T(8,128)S(1)} %bitcast.478, f32[3072,1536]{1,0:T(8,128)} %param.5), kind=kOutput, calls=%fused_computation.458 | convolution fusion | flops 14495514624 | bytes 28311552 | tf_op jit(solution)/shard_map/dot_general | solution.py:14
  134.4 18.4 %fusion.140 = f32[512,1536]{1,0:T(8,128)S(1)} fusion(f32[512,3072]{1,0:T(8,128)S(1)} %bitcast.475, f32[3072,1536]{1,0:T(8,128)} %param.5), kind=kOutput, calls=%fused_computation.459 | convolution fusion | flops 14495514624 | bytes 28311552 | tf_op jit(solution)/shard_map/dot_general | solution.py:14
  156.8 20.6 %fusion.138 = f32[512,1536]{1,0:T(8,128)S(1)} fusion(f32[512,3072]{1,0:T(8,128)S(1)} %bitcast.481, f32[3072,1536]{1,0:T(8,128)} %param.5), kind=kOutput, calls=%fused_computation.457 | convolution fusion | flops 14495514624 | bytes 28311552 | tf_op jit(solution)/shard_map/dot_general | solution.py:14
  179.9 2.9 fusion.1
  190.2 8.1 %collective-permute-done.8 = f32[2,128,768]{2,1,0:T(8,128)S(1)} collective-permute-done((f32[2,128,768]{2,1,0:T(8,128)S(1)}, f32[2,128,768]{2,1,0:T(8,128)S(1)}, u32[]{:S(2)}, u32[]{:S(2)}) %collective-permute-start.8) | collective-permute-done | bytes 786464 | tf_op jit(solution)/shard_map/ppermute | solution.py:25
  200.0 15.2 %collective-permute-done.10 = f32[2,128,768]{2,1,0:T(8,128)S(1)} collective-permute-done((f32[2,128,768]{2,1,0:T(8,128)S(1)}, f32[2,128,768]{2,1,0:T(8,128)S(1)}, u32[]{:S(2)}, u32[]{:S(2)}) %collective-permute-start.10) | collective-permute-done | bytes 786464 | tf_op jit(solution)/shard_map/ppermute | solution.py:25
  217.8 22.6 %collective-permute-done.19 = f32[2,128,768]{2,1,0:T(8,128)S(1)} collective-permute-done((f32[2,128,768]{2,1,0:T(8,128)S(1)}, f32[2,128,768]{2,1,0:T(8,128)S(1)}, u32[]{:S(2)}, u32[]{:S(2)}) %collective-permute-start.19) | collective-permute-done | bytes 786464 | tf_op jit(solution)/shard_map/ppermute | solution.py:25
  242.2 23.5 %collective-permute-done.21 = f32[2,128,768]{2,1,0:T(8,128)S(1)} collective-permute-done((f32[2,128,768]{2,1,0:T(8,128)S(1)}, f32[2,128,768]{2,1,0:T(8,128)S(1)}, u32[]{:S(2)}, u32[]{:S(2)}) %collective-permute-start.21) | collective-permute-done | bytes 786464 | tf_op jit(solution)/shard_map/ppermute | solution.py:25
  267.5 23.5 %collective-permute-done.30 = f32[2,128,768]{2,1,0:T(8,128)S(1)} collective-permute-done((f32[2,128,768]{2,1,0:T(8,128)S(1)}, f32[2,128,768]{2,1,0:T(8,128)S(1)}, u32[]{:S(2)}, u32[]{:S(2)}) %collective-permute-start.30) | collective-permute-done | bytes 786464 | tf_op jit(solution)/shard_map/ppermute | solution.py:25
  292.8 14.6 %collective-permute-done.32 = f32[2,128,768]{2,1,0:T(8,128)S(1)} collective-permute-done((f32[2,128,768]{2,1,0:T(8,128)S(1)}, f32[2,128,768]{2,1,0:T(8,128)S(1)}, u32[]{:S(2)}, u32[]{:S(2)}) %collective-permute-start.32) | collective-permute-done | bytes 786464 | tf_op jit(solution)/shard_map/ppermute | solution.py:25
  311.5 31.5 %collective-permute-done.22 = f32[1,128,768]{2,1,0:T(8,128)S(1)} collective-permute-done((f32[1,128,768]{2,1,0:T(8,128)S(1)}, f32[1,128,768]{2,1,0:T(8,128)S(1)}, u32[]{:S(2)}, u32[]{:S(2)}) %collective-permute-start.22) | collective-permute-done | bytes 393248 | tf_op jit(solution)/shard_map/ppermute | solution.py:25
  343.2 8.3 %collective-permute-done.31 = f32[1,128,768]{2,1,0:T(8,128)S(1)} collective-permute-done((f32[1,128,768]{2,1,0:T(8,128)S(1)}, f32[1,128,768]{2,1,0:T(8,128)S(1)}, u32[]{:S(2)}, u32[]{:S(2)}) %collective-permute-start.31) | collective-permute-done | bytes 393248 | tf_op jit(solution)/shard_map/ppermute | solution.py:25
  353.1 6.7 %collective-permute-done.33 = f32[1,128,768]{2,1,0:T(8,128)S(1)} collective-permute-done((f32[1,128,768]{2,1,0:T(8,128)S(1)}, f32[1,128,768]{2,1,0:T(8,128)S(1)}, u32[]{:S(2)}, u32[]{:S(2)}) %collective-permute-start.33) | collective-permute-done | bytes 393248 | tf_op jit(solution)/shard_map/ppermute | solution.py:25
  376.0 4.0 collective-permute-done.53
  398.9 5.5 %collective-permute-done.42 = f32[2,16,1536]{2,1,0:T(8,128)S(1)} collective-permute-done((f32[2,16,1536]{2,1,0:T(8,128)S(1)}, f32[2,16,1536]{2,1,0:T(8,128)S(1)}, u32[]{:S(2)}, u32[]{:S(2)}) %collective-permute-start.42) | collective-permute-done | bytes 196640 | tf_op jit(solution)/shard_map/ppermute | solution.py:25
  404.4 13.1 %collective-permute-start.75 = (f32[2,16,1536]{2,1,0:T(8,128)}, f32[2,16,1536]{2,1,0:T(8,128)}, u32[]{:S(2)}, u32[]{:S(2)}) collective-permute-start(f32[2,16,1536]{2,1,0:T(8,128)} %get-tuple-element.165), channel_id=1, source_target_pairs={{0,16},{8,24},{16,0},{24,8},{1,17},{9,25},{17,1},{25,9},{2,18},{10... | collective-permute-start | bytes 589832 | tf_op jit(solution)/shard_map/ppermute | solution.py:25
  421.1 5.8 %convolution_bitcast_fusion.5 = f32[2,2,16,1,512]{4,2,1,0,3:T(8,128)S(1)} fusion(f32[2,2,16,3072]{3,2,1,0:T(8,128)S(1)} %dot_general.67, f32[512,3072,1,1]{1,0,3,2:T(8,128)} %bitcast.482), kind=kOutput, calls=%fused_computation.98 | convolution fusion | flops 603979776 | bytes 7208960 | tf_op jit(solution)/shard_map/dot_general | solution.py:14
  426.9 5.8 %convolution_bitcast_fusion.4 = f32[2,2,16,1,512]{4,2,1,0,3:T(8,128)S(1)} fusion(f32[2,2,16,3072]{3,2,1,0:T(8,128)S(1)} %dot_general.67, f32[512,3072,1,1]{1,0,3,2:T(8,128)} %bitcast.479), kind=kOutput, calls=%fused_computation.97 | convolution fusion | flops 603979776 | bytes 7208960 | tf_op jit(solution)/shard_map/dot_general | solution.py:14
  440.6 5.8 %convolution_bitcast_fusion.3 = f32[2,2,16,1,512]{4,2,1,0,3:T(8,128)S(1)} fusion(f32[2,2,16,3072]{3,2,1,0:T(8,128)S(1)} %dot_general.73, f32[512,3072,1,1]{1,0,3,2:T(8,128)} %bitcast.480), kind=kOutput, calls=%fused_computation.96 | convolution fusion | flops 603979776 | bytes 7208960 | tf_op jit(solution)/shard_map/dot_general | solution.py:14
  446.4 6.0 %convolution_bitcast_fusion.2 = f32[2,2,16,1,512]{4,2,1,0,3:T(8,128)S(1)} fusion(f32[2,2,16,3072]{3,2,1,0:T(8,128)S(1)} %dot_general.73, f32[512,3072,1,1]{1,0,3,2:T(8,128)} %bitcast.476), kind=kOutput, calls=%fused_computation.95 | convolution fusion | flops 603979776 | bytes 7208960 | tf_op jit(solution)/shard_map/dot_general | solution.py:14
  457.9 5.8 %fusion.141 = f32[2,2,16,512]{3,2,1,0:T(8,128)S(1)} fusion(f32[2,2,16,3072]{3,2,1,0:T(8,128)S(1)} %dot_general.80, f32[512,3072,1,1]{1,0,3,2:T(8,128)} %bitcast.477), kind=kOutput, calls=%fused_computation.460 | convolution fusion | flops 603979776 | bytes 7208960 | tf_op jit(solution)/shard_map/dot_general | solution.py:14
  465.9 3.2 collective-permute-done.77
  470.6 3.5 collective-permute-done.78
  478.4 3.1 collective-permute-done.45
  485.6 3.3 collective-permute-done.81
  494.3 4.8 collective-permute-done.48
  517.1 3.4 collective-permute-done.84
  (342 shorter events, 155.6 us)
Async XLA Ops:
  8.1 33.8 %collective-permute-start.27 = (f32[64,3072]{1,0:T(8,128)S(1)}, f32[64,3072]{1,0:T(8,128)}, u32[]{:S(2)}, u32[]{:S(2)}) collective-permute-start(f32[64,3072]{1,0:T(8,128)S(1)} %get-tuple-element.216), channel_id=1, source_target_pairs={{0,2},{1,3},{2,0},{3,1},{4,6},{5,7},{6,4},{7,5},{8,10},{9,11},{10,... | collective-permute-start | bytes 2359304 | tf_op jit(solution)/shard_map/ppermute | solution.py:25
  9.2 34.7 %collective-permute-start.18 = (f32[64,3072]{1,0:T(8,128)S(1)}, f32[64,3072]{1,0:T(8,128)S(1)}, u32[]{:S(2)}, u32[]{:S(2)}) collective-permute-start(f32[64,3072]{1,0:T(8,128)S(1)} %get-tuple-element.217), channel_id=1, source_target_pairs={{0,1},{1,0},{2,3},{3,2},{4,5},{5,4},{6,7},{7,6},{8,9},{9,8},{10,11... | collective-permute-start | bytes 2359304 | tf_op jit(solution)/shard_map/ppermute | solution.py:25
  25.0 45.8 %collective-permute-start.25 = (f32[64,3072]{1,0:T(8,128)S(1)}, f32[64,3072]{1,0:T(8,128)S(1)}, u32[]{:S(2)}, u32[]{:S(2)}) collective-permute-start(f32[64,3072]{1,0:T(8,128)S(1)} %get-tuple-element.216), channel_id=1, source_target_pairs={{0,4},{1,5},{2,6},{3,7},{4,0},{5,1},{6,2},{7,3},{8,12},{9,13},{10,... | collective-permute-start | bytes 2359304 | tf_op jit(solution)/shard_map/ppermute | solution.py:25
  28.1 44.3 %collective-permute-start.23 = (f32[64,3072]{1,0:T(8,128)S(1)}, f32[64,3072]{1,0:T(8,128)S(1)}, u32[]{:S(2)}, u32[]{:S(2)}) collective-permute-start(f32[64,3072]{1,0:T(8,128)S(1)} %get-tuple-element.216), channel_id=1, source_target_pairs={{0,6},{1,7},{2,4},{3,5},{4,2},{5,3},{6,0},{7,1},{8,14},{9,15},{10,... | collective-permute-start | bytes 2359304 | tf_op jit(solution)/shard_map/ppermute | solution.py:25
  29.7 39.7 %collective-permute-start.3 = (f32[32,3072]{1,0:T(8,128)S(1)}, f32[32,3072]{1,0:T(8,128)S(1)}, u32[]{:S(2)}, u32[]{:S(2)}) collective-permute-start(f32[32,3072]{1,0:T(8,128)S(1)} %slice.188), channel_id=1, source_target_pairs={{0,4},{1,5},{2,6},{3,7},{4,0},{5,1},{6,2},{7,3},{8,12},{9,13},{10,... | collective-permute-start | bytes 1179656 | tf_op jit(solution)/shard_map/ppermute | solution.py:25
  41.9 25.0 %collective-permute-start.1 = (f32[32,3072]{1,0:T(8,128)S(1)}, f32[32,3072]{1,0:T(8,128)S(1)}, u32[]{:S(2)}, u32[]{:S(2)}) collective-permute-start(f32[32,3072]{1,0:T(8,128)S(1)} %slice.187), channel_id=1, source_target_pairs={{0,2},{1,3},{2,0},{3,1},{4,6},{5,7},{6,4},{7,5},{8,10},{9,11},{10,... | collective-permute-start | bytes 1179656 | tf_op jit(solution)/shard_map/ppermute | solution.py:25
  43.9 28.5 %collective-permute-start.28 = (f32[64,3072]{1,0:T(8,128)}, f32[64,3072]{1,0:T(8,128)S(1)}, u32[]{:S(2)}, u32[]{:S(2)}) collective-permute-start(f32[64,3072]{1,0:T(8,128)} %collective-permute-done.27), channel_id=1, source_target_pairs={{0,1},{1,0},{2,3},{3,2},{4,5},{5,4},{6,7},{7,6},{8,9},{9,8},{10,11... | collective-permute-start | bytes 2359304 | tf_op jit(solution)/shard_map/ppermute | solution.py:25
  69.3 35.0 %collective-permute-start.14 = (f32[64,3072]{1,0:T(8,128)S(1)}, f32[64,3072]{1,0:T(8,128)S(1)}, u32[]{:S(2)}, u32[]{:S(2)}) collective-permute-start(f32[64,3072]{1,0:T(8,128)S(1)} %get-tuple-element.217), channel_id=1, source_target_pairs={{0,4},{1,5},{2,6},{3,7},{4,0},{5,1},{6,2},{7,3},{8,12},{9,13},{10,... | collective-permute-start | bytes 2359304 | tf_op jit(solution)/shard_map/ppermute | solution.py:25
  70.9 33.5 %collective-permute-start.12 = (f32[64,3072]{1,0:T(8,128)S(1)}, f32[64,3072]{1,0:T(8,128)S(1)}, u32[]{:S(2)}, u32[]{:S(2)}) collective-permute-start(f32[64,3072]{1,0:T(8,128)S(1)} %get-tuple-element.217), channel_id=1, source_target_pairs={{0,6},{1,7},{2,4},{3,5},{4,2},{5,3},{6,0},{7,1},{8,14},{9,15},{10,... | collective-permute-start | bytes 2359304 | tf_op jit(solution)/shard_map/ppermute | solution.py:25
  72.4 32.5 %collective-permute-start.24 = (f32[64,3072]{1,0:T(8,128)S(1)}, f32[64,3072]{1,0:T(8,128)S(1)}, u32[]{:S(2)}, u32[]{:S(2)}) collective-permute-start(f32[64,3072]{1,0:T(8,128)S(1)} %collective-permute-done.23), channel_id=1, source_target_pairs={{0,1},{1,0},{2,3},{3,2},{4,5},{5,4},{6,7},{7,6},{8,9},{9,8},{10,11... | collective-permute-start | bytes 2359304 | tf_op jit(solution)/shard_map/ppermute | solution.py:25
  74.7 78.2 %collective-permute-start.6 = (f32[64,3072]{1,0:T(8,128)}, f32[64,3072]{1,0:T(8,128)S(1)}, u32[]{:S(2)}, u32[]{:S(2)}) collective-permute-start(f32[64,3072]{1,0:T(8,128)} %collective-permute-done.2), channel_id=1, source_target_pairs={{0,1},{1,0},{2,3},{3,2},{4,5},{5,4},{6,7},{7,6},{8,9},{9,8},{10,11... | collective-permute-start | bytes 2359304 | tf_op jit(solution)/shard_map/ppermute | solution.py:25
  87.4 67.1 %collective-permute-start.5 = (f32[64,3072]{1,0:T(8,128)S(1)}, f32[64,3072]{1,0:T(8,128)S(1)}, u32[]{:S(2)}, u32[]{:S(2)}) collective-permute-start(f32[64,3072]{1,0:T(8,128)S(1)} %collective-permute-done), channel_id=1, source_target_pairs={{0,1},{1,0},{2,3},{3,2},{4,5},{5,4},{6,7},{7,6},{8,9},{9,8},{10,11... | collective-permute-start | bytes 2359304 | tf_op jit(solution)/shard_map/ppermute | solution.py:25
  107.0 47.7 %collective-permute-start.4 = (f32[64,3072]{1,0:T(8,128)S(1)}, f32[64,3072]{1,0:T(8,128)S(1)}, u32[]{:S(2)}, u32[]{:S(2)}) collective-permute-start(f32[64,3072]{1,0:T(8,128)S(1)} %constant_dynamic-update-slice_fusion), channel_id=1, source_target_pairs={{0,1},{1,0},{2,3},{3,2},{4,5},{5,4},{6,7},{7,6},{8,9},{9,8},{10,11... | collective-permute-start | bytes 2359304 | tf_op jit(solution)/shard_map/ppermute | solution.py:25
  179.4 35.8 %collective-permute-start.10 = (f32[2,128,768]{2,1,0:T(8,128)S(1)}, f32[2,128,768]{2,1,0:T(8,128)S(1)}, u32[]{:S(2)}, u32[]{:S(2)}) collective-permute-start(f32[2,128,768]{2,1,0:T(8,128)S(1)} %dynamic-slice_bitcast_fusion.4), channel_id=1, source_target_pairs={{0,8},{8,0},{16,24},{24,16},{1,9},{9,1},{17,25},{25,17},{2,10},{10... | collective-permute-start | bytes 2359304 | tf_op jit(solution)/shard_map/ppermute | solution.py:25
  186.3 54.1 %collective-permute-start.19 = (f32[2,128,768]{2,1,0:T(8,128)S(1)}, f32[2,128,768]{2,1,0:T(8,128)S(1)}, u32[]{:S(2)}, u32[]{:S(2)}) collective-permute-start(f32[2,128,768]{2,1,0:T(8,128)S(1)} %dynamic-slice_bitcast_fusion.3), channel_id=1, source_target_pairs={{0,8},{8,0},{16,24},{24,16},{1,9},{9,1},{17,25},{25,17},{2,10},{10... | collective-permute-start | bytes 2359304 | tf_op jit(solution)/shard_map/ppermute | solution.py:25
  188.1 77.6 %collective-permute-start.21 = (f32[2,128,768]{2,1,0:T(8,128)S(1)}, f32[2,128,768]{2,1,0:T(8,128)S(1)}, u32[]{:S(2)}, u32[]{:S(2)}) collective-permute-start(f32[2,128,768]{2,1,0:T(8,128)S(1)} %dynamic-slice_bitcast_fusion.2), channel_id=1, source_target_pairs={{0,8},{8,0},{16,24},{24,16},{1,9},{9,1},{17,25},{25,17},{2,10},{10... | collective-permute-start | bytes 2359304 | tf_op jit(solution)/shard_map/ppermute | solution.py:25
  188.7 102.3 %collective-permute-start.30 = (f32[2,128,768]{2,1,0:T(8,128)S(1)}, f32[2,128,768]{2,1,0:T(8,128)S(1)}, u32[]{:S(2)}, u32[]{:S(2)}) collective-permute-start(f32[2,128,768]{2,1,0:T(8,128)S(1)} %dynamic-slice_bitcast_fusion.1), channel_id=1, source_target_pairs={{0,8},{8,0},{16,24},{24,16},{1,9},{9,1},{17,25},{25,17},{2,10},{10... | collective-permute-start | bytes 2359304 | tf_op jit(solution)/shard_map/ppermute | solution.py:25
  198.3 109.1 %collective-permute-start.32 = (f32[2,128,768]{2,1,0:T(8,128)S(1)}, f32[2,128,768]{2,1,0:T(8,128)S(1)}, u32[]{:S(2)}, u32[]{:S(2)}) collective-permute-start(f32[2,128,768]{2,1,0:T(8,128)S(1)} %dynamic-slice_bitcast_fusion), channel_id=1, source_target_pairs={{0,8},{8,0},{16,24},{24,16},{1,9},{9,1},{17,25},{25,17},{2,10},{10... | collective-permute-start | bytes 2359304 | tf_op jit(solution)/shard_map/ppermute | solution.py:25
  215.2 94.0 %collective-permute-start.9 = (f32[1,128,768]{2,1,0:T(8,128)S(1)}, f32[1,128,768]{2,1,0:T(8,128)S(1)}, u32[]{:S(2)}, u32[]{:S(2)}) collective-permute-start(f32[1,128,768]{2,1,0:T(8,128)S(1)} %constant_dynamic-slice_fusion.17), channel_id=1, source_target_pairs={{0,16},{8,24},{16,0},{24,8},{1,17},{9,25},{17,1},{25,9},{2,18},{10... | collective-permute-start | bytes 1179656 | tf_op jit(solution)/shard_map/ppermute | solution.py:25
  240.4 70.2 %collective-permute-start.11 = (f32[1,128,768]{2,1,0:T(8,128)S(1)}, f32[1,128,768]{2,1,0:T(8,128)S(1)}, u32[]{:S(2)}, u32[]{:S(2)}) collective-permute-start(f32[1,128,768]{2,1,0:T(8,128)S(1)} %constant_dynamic-slice_fusion.15), channel_id=1, source_target_pairs={{0,16},{8,24},{16,0},{24,8},{1,17},{9,25},{17,1},{25,9},{2,18},{10... | collective-permute-start | bytes 1179656 | tf_op jit(solution)/shard_map/ppermute | solution.py:25
  265.7 45.2 %collective-permute-start.20 = (f32[1,128,768]{2,1,0:T(8,128)S(1)}, f32[1,128,768]{2,1,0:T(8,128)S(1)}, u32[]{:S(2)}, u32[]{:S(2)}) collective-permute-start(f32[1,128,768]{2,1,0:T(8,128)S(1)} %constant_dynamic-slice_fusion.14), channel_id=1, source_target_pairs={{0,16},{8,24},{16,0},{24,8},{1,17},{9,25},{17,1},{25,9},{2,18},{10... | collective-permute-start | bytes 1179656 | tf_op jit(solution)/shard_map/ppermute | solution.py:25
  291.0 52.0 %collective-permute-start.22 = (f32[1,128,768]{2,1,0:T(8,128)S(1)}, f32[1,128,768]{2,1,0:T(8,128)S(1)}, u32[]{:S(2)}, u32[]{:S(2)}) collective-permute-start(f32[1,128,768]{2,1,0:T(8,128)S(1)} %constant_dynamic-slice_fusion.13), channel_id=1, source_target_pairs={{0,16},{8,24},{16,0},{24,8},{1,17},{9,25},{17,1},{25,9},{2,18},{10... | collective-permute-start | bytes 1179656 | tf_op jit(solution)/shard_map/ppermute | solution.py:25
  307.4 44.1 %collective-permute-start.31 = (f32[1,128,768]{2,1,0:T(8,128)S(1)}, f32[1,128,768]{2,1,0:T(8,128)S(1)}, u32[]{:S(2)}, u32[]{:S(2)}) collective-permute-start(f32[1,128,768]{2,1,0:T(8,128)S(1)} %constant_dynamic-slice_fusion.12), channel_id=1, source_target_pairs={{0,16},{8,24},{16,0},{24,8},{1,17},{9,25},{17,1},{25,9},{2,18},{10... | collective-permute-start | bytes 1179656 | tf_op jit(solution)/shard_map/ppermute | solution.py:25
  309.2 50.6 %collective-permute-start.33 = (f32[1,128,768]{2,1,0:T(8,128)S(1)}, f32[1,128,768]{2,1,0:T(8,128)S(1)}, u32[]{:S(2)}, u32[]{:S(2)}) collective-permute-start(f32[1,128,768]{2,1,0:T(8,128)S(1)} %constant_dynamic-slice_fusion.11), channel_id=1, source_target_pairs={{0,16},{8,24},{16,0},{24,8},{1,17},{9,25},{17,1},{25,9},{2,18},{10... | collective-permute-start | bytes 1179656 | tf_op jit(solution)/shard_map/ppermute | solution.py:25
  310.9 52.1 %collective-permute-start.34 = (f32[16,1536]{1,0:T(8,128)S(1)}, f32[16,1536]{1,0:T(8,128)S(1)}, u32[]{:S(2)}, u32[]{:S(2)}) collective-permute-start(f32[16,1536]{1,0:T(8,128)S(1)} %get-tuple-element.92), channel_id=1, source_target_pairs={{0,1},{1,0},{2,3},{3,2},{4,5},{5,4},{6,7},{7,6},{8,9},{9,8},{10,11... | collective-permute-start | bytes 294920 | tf_op jit(solution)/shard_map/ppermute | solution.py:25
  310.9 52.9 %collective-permute-start.35 = (f32[16,1536]{1,0:T(8,128)S(1)}, f32[16,1536]{1,0:T(8,128)S(1)}, u32[]{:S(2)}, u32[]{:S(2)}) collective-permute-start(f32[16,1536]{1,0:T(8,128)S(1)} %get-tuple-element.93), channel_id=1, source_target_pairs={{0,2},{1,3},{2,0},{3,1},{4,6},{5,7},{6,4},{7,5},{8,10},{9,11},{10,... | collective-permute-start | bytes 294920 | tf_op jit(solution)/shard_map/ppermute | solution.py:25
  343.0 22.7 %collective-permute-start.36 = (f32[16,1536]{1,0:T(8,128)S(1)}, f32[16,1536]{1,0:T(8,128)S(1)}, u32[]{:S(2)}, u32[]{:S(2)}) collective-permute-start(f32[16,1536]{1,0:T(8,128)S(1)} %get-tuple-element.94), channel_id=1, source_target_pairs={{0,3},{1,2},{2,1},{3,0},{4,7},{5,6},{6,5},{7,4},{8,11},{9,10},{10,... | collective-permute-start | bytes 294920 | tf_op jit(solution)/shard_map/ppermute | solution.py:25
  391.6 41.0 %collective-permute-start.56 = (f32[2,16,1536]{2,1,0:T(8,128)}, f32[2,16,1536]{2,1,0:T(8,128)}, u32[]{:S(2)}, u32[]{:S(2)}) collective-permute-start(f32[2,16,1536]{2,1,0:T(8,128)} %get-tuple-element.132), channel_id=1, source_target_pairs={{0,8},{8,0},{16,24},{24,16},{1,9},{9,1},{17,25},{25,17},{2,10},{10... | collective-permute-start | bytes 589832 | tf_op jit(solution)/shard_map/ppermute | solution.py:25
  391.9 43.3 %collective-permute-start.57 = (f32[2,16,1536]{2,1,0:T(8,128)}, f32[2,16,1536]{2,1,0:T(8,128)}, u32[]{:S(2)}, u32[]{:S(2)}) collective-permute-start(f32[2,16,1536]{2,1,0:T(8,128)} %get-tuple-element.133), channel_id=1, source_target_pairs={{0,16},{8,24},{16,0},{24,8},{1,17},{9,25},{17,1},{25,9},{2,18},{10... | collective-permute-start | bytes 589832 | tf_op jit(solution)/shard_map/ppermute | solution.py:25
  397.6 37.5 %collective-permute-start.58 = (f32[2,16,1536]{2,1,0:T(8,128)S(1)}, f32[2,16,1536]{2,1,0:T(8,128)}, u32[]{:S(2)}, u32[]{:S(2)}) collective-permute-start(f32[2,16,1536]{2,1,0:T(8,128)S(1)} %get-tuple-element.134), channel_id=1, source_target_pairs={{0,24},{8,16},{16,8},{24,0},{1,25},{9,17},{17,9},{25,1},{2,26},{10... | collective-permute-start | bytes 589832 | tf_op jit(solution)/shard_map/ppermute | solution.py:25
  404.4 48.0 %collective-permute-start.74 = (f32[2,16,1536]{2,1,0:T(8,128)}, f32[2,16,1536]{2,1,0:T(8,128)}, u32[]{:S(2)}, u32[]{:S(2)}) collective-permute-start(f32[2,16,1536]{2,1,0:T(8,128)} %get-tuple-element.164), channel_id=1, source_target_pairs={{0,8},{8,0},{16,24},{24,16},{1,9},{9,1},{17,25},{25,17},{2,10},{10... | collective-permute-start | bytes 589832 | tf_op jit(solution)/shard_map/ppermute | solution.py:25
  404.4 48.0 %collective-permute-start.75 = (f32[2,16,1536]{2,1,0:T(8,128)}, f32[2,16,1536]{2,1,0:T(8,128)}, u32[]{:S(2)}, u32[]{:S(2)}) collective-permute-start(f32[2,16,1536]{2,1,0:T(8,128)} %get-tuple-element.165), channel_id=1, source_target_pairs={{0,16},{8,24},{16,0},{24,8},{1,17},{9,25},{17,1},{25,9},{2,18},{10... | collective-permute-start | bytes 589832 | tf_op jit(solution)/shard_map/ppermute | solution.py:25
  (60 other events, 555.5 us)
